TPU v7x, 256 devices: a whole 4x4x8 slice. The times are simulated.
256 devices in a mesh: row: 8 (over y, core), col: 32 (over x, z).
Axes of the slice: x: 4, y: 4, z: 8, core: 2. Of those that a mesh axis runs over, the one named last changes fastest.
Arguments:
- x_blocks: bfloat16 [8, 32, 42, 128, 128], P('row', 'col'), may hold values from -1.1953125 to 1.1953125
- x_slots: int32 [8, 32, 42], replicated, may hold values from 0 to 255, as said below
- x_count: int32 [8, 32], replicated, may hold values from 21 to 42, as said below
- s_slots: int32 [8, 32, 2], replicated, may hold values from 0 to 15, as said below
- s_count: int32 [8, 32], replicated, may hold values from 1 to 2, as said below
Outputs:
- square_blocks: bfloat16 [8, 32, 2, 128, 128], P('row', 'col')
- result_blocks: bfloat16 [8, 32, 2, 128, 128], P('row', 'col')
Inputs may be any that keep to these rules, and one draw needn't show every extreme that they name: `x_slots`: in each tile the live slots hold distinct positions; the live blocks whose position % 32 is below 2 come first among the live slots, at most 2 of them, and some tile has exactly 2. Positions of slots that are not live are arbitrary within the range. `x_count`: some tile has exactly 42 live slots. `s_slots`: in each tile the live slots hold distinct positions. `s_count`: some tile has exactly 2 live slots.
All inputs are finite; a program needn't handle non-finite values.
Results may differ from a plain program's by a relative error of at most 0.0049.
Values may be sent and summed in bfloat16 or wider, within the bound.
A program may use at most 128 MiB of HBM per device.

v0:
```python
import math
import jax
import jax.numpy as jnp
from jax import lax
from jax.sharding import PartitionSpec as P

RB = 8
JW = 2
CAPW = 2


def laid_out(pieces, dim):
    dims = list(pieces.shape[1:])
    dims[dim] *= pieces.shape[0]
    return jnp.moveaxis(pieces, 0, dim).reshape(dims)


def copy_for_each(array, axis):
    length = lax.axis_size(axis)
    return lax.all_to_all(
        jnp.broadcast_to(array[None], (length, *array.shape)), axis, 0, 0, tiled=True
    )


def gathered_copies(array, axis, dim):
    return laid_out(copy_for_each(array, axis), dim)


def match_index(targets, slot_keys, slot_live):
    matches = (targets[..., None] == slot_keys) & slot_live
    ordinal = jnp.arange(1, slot_keys.shape[0] + 1, dtype=jnp.int32)
    located = jnp.sum(jnp.where(matches, ordinal, 0), axis=-1)
    return jnp.where(located > 0, located - 1, slot_keys.shape[0])


def local(x_blocks, x_slots, x_count, s_slots, s_count):
    row_total = lax.axis_size("row")
    col_total = lax.axis_size("col")
    row_id = lax.axis_index("row")
    col_id = lax.axis_index("col")
    capacity = x_blocks.shape[2]
    block_size = x_blocks.shape[3]
    order_blocks = RB * col_total
    tile_width = order_blocks // row_total
    panel_all = lax.all_gather(x_blocks, "row", axis=0, tiled=True)
    stacked = panel_all.reshape(row_total * capacity, block_size, block_size)
    padded = jnp.concatenate(
        [stacked, jnp.zeros((1, block_size, block_size), stacked.dtype)], axis=0
    )
    column_slots = lax.dynamic_index_in_dim(x_slots, col_id, 1, keepdims=False)
    column_count = lax.dynamic_index_in_dim(x_count, col_id, 1, keepdims=False)
    ordinal = jnp.arange(capacity, dtype=jnp.int32)
    panel_live = (ordinal[None, :] < column_count[:, None]).reshape(-1)
    owners = jnp.arange(row_total, dtype=jnp.int32)[:, None]
    panel_keys = (
        column_slots // tile_width * order_blocks + owners * tile_width + column_slots % tile_width
    ).reshape(-1)
    row_lanes = jnp.arange(RB, dtype=jnp.int32)
    window_ids = jnp.arange(JW, dtype=jnp.int32)

    def accumulate(running, values, inner_row, inner_col, usable):
        picked = match_index(
            row_lanes[None, :] * order_blocks + inner_row[:, None], panel_keys, panel_live
        )
        left_part = jnp.take(padded, picked, axis=0)
        placing = ((inner_col[:, None] == window_ids[None, :]) & usable[:, None]).astype(
            values.dtype
        )
        placed = placing[:, :, None, None] * values[:, None, :, :]
        return running + jnp.einsum(
            "nrxy,njyz->rjxz", left_part, placed, preferred_element_type=jnp.float32
        )

    def make_step(slot_table, count_row, stride, column_limit):

        def fold_step(running, piece, offset):
            pieces = piece.shape[1]
            slot_count = piece.shape[2]
            positions = lax.dynamic_slice_in_dim(slot_table, offset, pieces, 0)[:, :slot_count]
            counts = lax.dynamic_slice_in_dim(count_row, offset, pieces, 0)
            owner_ids = offset + jnp.arange(pieces, dtype=jnp.int32)[:, None]
            inner_row = owner_ids * RB + positions // stride
            inner_col = positions % stride
            usable = (jnp.arange(slot_count, dtype=jnp.int32)[None, :] < counts[:, None]) & (
                inner_col < column_limit
            )
            values = piece.reshape(pieces * slot_count, block_size, block_size)
            return accumulate(
                running, values, inner_row.reshape(-1), inner_col.reshape(-1), usable.reshape(-1)
            )

        return fold_step

    blank_sum = jnp.zeros((RB, JW, block_size, block_size), jnp.float32)

    def collect_all(gathered, fold_step):
        per_turn = math.gcd(col_total, 8)

        def advance(turn_index, running):
            offset = turn_index * per_turn
            portion = lax.dynamic_slice_in_dim(gathered, offset, per_turn, 1)
            return fold_step(running, portion, offset)

        return lax.fori_loop(0, col_total // per_turn, advance, blank_sum)

    row_slots = lax.dynamic_index_in_dim(x_slots, row_id, 0, keepdims=False)
    row_count = lax.dynamic_index_in_dim(x_count, row_id, 0, keepdims=False)
    square_slots = lax.dynamic_index_in_dim(s_slots, row_id, 0, keepdims=False)
    square_count = lax.dynamic_index_in_dim(s_count, row_id, 0, keepdims=False)
    window_part = x_blocks[:, :, :CAPW]
    first_step = make_step(row_slots, row_count, tile_width, JW)
    product = collect_all(gathered_copies(window_part, "col", 1), first_step)
    own_slots = lax.dynamic_index_in_dim(square_slots, col_id, 0, keepdims=False)
    own_count = lax.dynamic_index_in_dim(square_count, col_id, 0, keepdims=False)
    own_live = jnp.arange(own_slots.shape[0], dtype=jnp.int32) < own_count
    flat_one = product.reshape(RB * JW, block_size, block_size)
    square_part = jnp.where(
        own_live[:, None, None], jnp.take(flat_one, own_slots, axis=0), 0.0
    ).astype(jnp.bfloat16)
    square_part = square_part[None, None]
    second_step = make_step(square_slots, square_count, JW, JW)
    second = collect_all(gathered_copies(square_part, "col", 1), second_step)
    own_keys = own_slots // JW * order_blocks + row_id * tile_width + own_slots % JW
    own_block = jnp.take(padded, match_index(own_keys, panel_keys, panel_live), axis=0).astype(
        jnp.float32
    )
    flat_two = second.reshape(RB * JW, block_size, block_size)
    combined = 1.5 * own_block - 0.5 * jnp.take(flat_two, own_slots, axis=0)
    result = jnp.where(own_live[:, None, None], combined, 0.0).astype(jnp.bfloat16)
    return (square_part, result[None, None])


def solution(mesh):
    in_specs = (P("row", "col", None, None, None), P(), P(), P(), P())
    out_specs = (P("row", "col", None, None, None), P("row", "col", None, None, None))
    return jax.shard_map(local, mesh=mesh, in_specs=in_specs, out_specs=out_specs, check_vma=False)
```

profile of v0, /device:TPU:1, one launch (start us, length us, event | category | flops | bytes accessed | tf_op | source)
XLA Modules:
  0.0 268.8 jit_solution(12169378988364675214)
XLA Ops:
  7.9 0.8 slice_bitcast_fusion
  8.9 1.9 broadcast_in_dim.199
  10.8 11.9 %all-to-all-start = ((bf16[32,1,1,2,128,128]{4,5,3,2,1,0:T(8,128)(2,1)}), bf16[32,1,1,2,128,128]{4,5,3,2,1,0:T(8,128)(2,1)S(1)}, u32[]{:S(2)}, u32[]{:S(2)}) async-start(bf16[32,1,1,2,128,128]{4,5,3,2,1,0:T(8,128)(2,1)} %broadcast_in_dim.199), calls=%async_computation | async-start | bytes 4194304 | tf_op jit(solution)/shard_map/all_to_all | solution.py:20
  23.2 1.4 fusion.74
  25.5 1.3 dynamic_slice.97
  28.4 48.9 %all-gather.2.cloned.1.call-done = bf16[8,1,42,128,128]{4,3,2,1,0:T(8,128)(2,1)} async-done(((bf16[1,1,42,128,128]{4,3,2,1,0:T(8,128)(2,1)}), bf16[8,1,42,128,128]{4,3,2,1,0:T(8,128)(2,1)}) %all-gather.2.cloned.1.call-update) | async-done | bytes 11010064 | tf_op jit(solution)/shard_map/all_gather | solution.py:45
  77.3 10.6 %concatenate.3 = bf16[337,128,128]{2,1,0:T(8,128)(2,1)} pad(bf16[336,128,128]{2,1,0:T(8,128)(2,1)} %bitcast.101, bf16[]{:T(256)} %constant.410.clone.1), padding=0_1x0_0x0_0 | pad | bytes 22052866 | tf_op jit(solution)/shard_map/concatenate | solution.py:47
  87.9 54.0 %while.36 = (s32[]{:T(128)}, f32[8,2,128,128]{2,3,0,1:T(8,128)}, s32[32,42]{1,0:T(8,128)S(1)}, s32[32]{0:T(128)S(1)}, bf16[1,32,2,128,128]{3,4,2,1,0:T(8,128)(2,...) while((s32[]{:T(128)}, f32[8,2,128,128]{2,3,0,1:T(8,128)}, ...), condition=%wide.wide.region_2.4_spmd.clone, body=%wide.wide.region_0.3_spmd.clone.sunk | while | flops 1078636672 | bytes 16272037 | solution.py:104
  89.0 7.3 %gather_fusion = bf16[128,128,128]{2,1,0:T(8,128)(2,1)} fusion(bf16[337,128,128]{2,1,0:T(8,128)(2,1)} %get-tuple-element.924, s32[1024]{0:T(1024)S(1)} %pad_clamp_fusion.8), kind=kCustom, calls=%fused_computation.clone.clone.clone.1 | custom fusion | bytes 8389120 | tf_op jit(solution)/shard_map/while/body/eval_jaxpr/jit(_take)/gather | solution.py:65
  96.6 4.6 %fusion.100 = f32[8,2,128,128]{2,3,0,1:T(8,128)} fusion(bf16[16,8,128,128]{3,2,1,0:T(8,128)(2,1)} %bitcast.97, pred[16,8]{0,1:T(8,128)(4,1)S(1)} %copy.73, f32[8,2,128,128]{2,3,0,1:T(8,128)} %get-tuple-element.906, bf16[16,128,128]{1,2,0:T(8,128)(2,1)S(1)} %bitcast.99, bf16[16,2]{0,1:T(2,128)(2,1)S(1)} %and_convert_fusion.6, pred[]{:T(512)S(6)} %compare.58), kind=kOutput, calls=%fused_computation.17.clone.clone.1 | convolution fusion | flops 1078460416 | bytes 6815937 | tf_op jit(solution)/shard_map/while/body/eval_jaxpr/nrxy,njyz->rjxz/dot_general | solution.py:70
  102.3 7.3 %gather_fusion = bf16[128,128,128]{2,1,0:T(8,128)(2,1)} fusion(bf16[337,128,128]{2,1,0:T(8,128)(2,1)} %get-tuple-element.924, s32[1024]{0:T(1024)S(1)} %pad_clamp_fusion.8), kind=kCustom, calls=%fused_computation.clone.clone.clone.1 | custom fusion | bytes 8389120 | tf_op jit(solution)/shard_map/while/body/eval_jaxpr/jit(_take)/gather | solution.py:65
  109.9 4.8 %fusion.100 = f32[8,2,128,128]{2,3,0,1:T(8,128)} fusion(bf16[16,8,128,128]{3,2,1,0:T(8,128)(2,1)} %bitcast.97, pred[16,8]{0,1:T(8,128)(4,1)S(1)} %copy.73, f32[8,2,128,128]{2,3,0,1:T(8,128)} %get-tuple-element.906, bf16[16,128,128]{1,2,0:T(8,128)(2,1)S(1)} %bitcast.99, bf16[16,2]{0,1:T(2,128)(2,1)S(1)} %and_convert_fusion.6, pred[]{:T(512)S(6)} %compare.58), kind=kOutput, calls=%fused_computation.17.clone.clone.1 | convolution fusion | flops 1078460416 | bytes 6815937 | tf_op jit(solution)/shard_map/while/body/eval_jaxpr/nrxy,njyz->rjxz/dot_general | solution.py:70
  115.9 7.3 %gather_fusion = bf16[128,128,128]{2,1,0:T(8,128)(2,1)} fusion(bf16[337,128,128]{2,1,0:T(8,128)(2,1)} %get-tuple-element.924, s32[1024]{0:T(1024)S(1)} %pad_clamp_fusion.8), kind=kCustom, calls=%fused_computation.clone.clone.clone.1 | custom fusion | bytes 8389120 | tf_op jit(solution)/shard_map/while/body/eval_jaxpr/jit(_take)/gather | solution.py:65
  123.5 4.8 %fusion.100 = f32[8,2,128,128]{2,3,0,1:T(8,128)} fusion(bf16[16,8,128,128]{3,2,1,0:T(8,128)(2,1)} %bitcast.97, pred[16,8]{0,1:T(8,128)(4,1)S(1)} %copy.73, f32[8,2,128,128]{2,3,0,1:T(8,128)} %get-tuple-element.906, bf16[16,128,128]{1,2,0:T(8,128)(2,1)S(1)} %bitcast.99, bf16[16,2]{0,1:T(2,128)(2,1)S(1)} %and_convert_fusion.6, pred[]{:T(512)S(6)} %compare.58), kind=kOutput, calls=%fused_computation.17.clone.clone.1 | convolution fusion | flops 1078460416 | bytes 6815937 | tf_op jit(solution)/shard_map/while/body/eval_jaxpr/nrxy,njyz->rjxz/dot_general | solution.py:70
  129.4 7.3 %gather_fusion = bf16[128,128,128]{2,1,0:T(8,128)(2,1)} fusion(bf16[337,128,128]{2,1,0:T(8,128)(2,1)} %get-tuple-element.924, s32[1024]{0:T(1024)S(1)} %pad_clamp_fusion.8), kind=kCustom, calls=%fused_computation.clone.clone.clone.1 | custom fusion | bytes 8389120 | tf_op jit(solution)/shard_map/while/body/eval_jaxpr/jit(_take)/gather | solution.py:65
  137.0 4.8 %fusion.100 = f32[8,2,128,128]{2,3,0,1:T(8,128)} fusion(bf16[16,8,128,128]{3,2,1,0:T(8,128)(2,1)} %bitcast.97, pred[16,8]{0,1:T(8,128)(4,1)S(1)} %copy.73, f32[8,2,128,128]{2,3,0,1:T(8,128)} %get-tuple-element.906, bf16[16,128,128]{1,2,0:T(8,128)(2,1)S(1)} %bitcast.99, bf16[16,2]{0,1:T(2,128)(2,1)S(1)} %and_convert_fusion.6, pred[]{:T(512)S(6)} %compare.58), kind=kOutput, calls=%fused_computation.17.clone.clone.1 | convolution fusion | flops 1078460416 | bytes 6815937 | tf_op jit(solution)/shard_map/while/body/eval_jaxpr/nrxy,njyz->rjxz/dot_general | solution.py:70
  141.9 1.5 copy.37
  144.2 1.9 broadcast_in_dim.207
  146.0 9.6 %all-to-all-start.1 = ((bf16[32,1,1,2,128,128]{4,5,3,2,1,0:T(8,128)(2,1)}), bf16[32,1,1,2,128,128]{4,5,3,2,1,0:T(8,128)(2,1)S(1)}, u32[]{:S(2)}, u32[]{:S(2)}) async-start(bf16[32,1,1,2,128,128]{4,5,3,2,1,0:T(8,128)(2,1)} %broadcast_in_dim.207), calls=%async_computation.1 | async-start | bytes 4194304 | tf_op jit(solution)/shard_map/all_to_all | solution.py:20
  156.4 4.7 %gather_fusion.2 = bf16[2,128,128]{2,1,0:T(8,128)(2,1)S(1)} fusion(bf16[337,128,128]{2,1,0:T(8,128)(2,1)} %get-tuple-element.971, s32[1024]{0:T(1024)S(1)} %pad_clamp_fusion.2), kind=kCustom, calls=%fused_computation.4 | custom fusion | bytes 131080 | tf_op jit(solution)/shard_map/jit(_take)/gather | solution.py:124
  161.8 42.7 %all-to-all-done.1 = bf16[32,1,1,2,128,128]{4,5,3,2,1,0:T(8,128)(2,1)S(1)} async-done(((bf16[32,1,1,2,128,128]{4,5,3,2,1,0:T(8,128)(2,1)}), bf16[32,1,1,2,128,128]{4,5,3,2,1,0:T(8,128)(2,1)S(1)}, u32[]{:S(2)}, u32[]{:S(2)}) %all-to-all-start.1) | async-done | bytes 2097184 | tf_op jit(solution)/shard_map/all_to_all | solution.py:20
  204.5 54.6 %while.37 = (s32[]{:T(128)}, f32[8,2,128,128]{2,3,0,1:T(8,128)}, s32[32,2]{0,1:T(2,128)S(1)}, s32[32]{0:T(128)S(1)}, bf16[1,32,2,128,128]{3,4,2,1,0:T(8,128)(2,1...) while((s32[]{:T(128)}, f32[8,2,128,128]{2,3,0,1:T(8,128)}, ...), condition=%wide.wide.region_6.9_spmd.clone, body=%wide.wide.region_4.8_spmd.clone.sunk | while | flops 1078636672 | bytes 16269573 | solution.py:104
  206.0 7.3 %gather_fusion.1 = bf16[128,128,128]{2,1,0:T(8,128)(2,1)} fusion(bf16[337,128,128]{2,1,0:T(8,128)(2,1)} %get-tuple-element.963, s32[1024]{0:T(1024)S(1)} %pad_clamp_fusion.9), kind=kCustom, calls=%fused_computation.2.clone.clone.clone.1 | custom fusion | bytes 8389120 | tf_op jit(solution)/shard_map/while/body/eval_jaxpr/jit(_take)/gather | solution.py:65
  213.4 4.6 %fusion.105 = f32[8,2,128,128]{2,3,0,1:T(8,128)} fusion(bf16[16,8,128,128]{3,2,1,0:T(8,128)(2,1)} %bitcast.98, pred[16,8]{0,1:T(8,128)(4,1)S(1)} %copy.76, f32[8,2,128,128]{2,3,0,1:T(8,128)} %get-tuple-element.945, bf16[16,128,128]{1,2,0:T(8,128)(2,1)S(1)} %bitcast.100, bf16[16,2]{0,1:T(2,128)(2,1)S(1)} %and_convert_fusion.7, pred[]{:T(512)S(6)} %compare.59), kind=kOutput, calls=%fused_computation.53.clone.clone.1 | convolution fusion | flops 1078460416 | bytes 6815937 | tf_op jit(solution)/shard_map/while/body/eval_jaxpr/nrxy,njyz->rjxz/dot_general | solution.py:70
  219.4 7.3 %gather_fusion.1 = bf16[128,128,128]{2,1,0:T(8,128)(2,1)} fusion(bf16[337,128,128]{2,1,0:T(8,128)(2,1)} %get-tuple-element.963, s32[1024]{0:T(1024)S(1)} %pad_clamp_fusion.9), kind=kCustom, calls=%fused_computation.2.clone.clone.clone.1 | custom fusion | bytes 8389120 | tf_op jit(solution)/shard_map/while/body/eval_jaxpr/jit(_take)/gather | solution.py:65
  226.8 4.8 %fusion.105 = f32[8,2,128,128]{2,3,0,1:T(8,128)} fusion(bf16[16,8,128,128]{3,2,1,0:T(8,128)(2,1)} %bitcast.98, pred[16,8]{0,1:T(8,128)(4,1)S(1)} %copy.76, f32[8,2,128,128]{2,3,0,1:T(8,128)} %get-tuple-element.945, bf16[16,128,128]{1,2,0:T(8,128)(2,1)S(1)} %bitcast.100, bf16[16,2]{0,1:T(2,128)(2,1)S(1)} %and_convert_fusion.7, pred[]{:T(512)S(6)} %compare.59), kind=kOutput, calls=%fused_computation.53.clone.clone.1 | convolution fusion | flops 1078460416 | bytes 6815937 | tf_op jit(solution)/shard_map/while/body/eval_jaxpr/nrxy,njyz->rjxz/dot_general | solution.py:70
  233.1 7.3 %gather_fusion.1 = bf16[128,128,128]{2,1,0:T(8,128)(2,1)} fusion(bf16[337,128,128]{2,1,0:T(8,128)(2,1)} %get-tuple-element.963, s32[1024]{0:T(1024)S(1)} %pad_clamp_fusion.9), kind=kCustom, calls=%fused_computation.2.clone.clone.clone.1 | custom fusion | bytes 8389120 | tf_op jit(solution)/shard_map/while/body/eval_jaxpr/jit(_take)/gather | solution.py:65
  240.5 4.8 %fusion.105 = f32[8,2,128,128]{2,3,0,1:T(8,128)} fusion(bf16[16,8,128,128]{3,2,1,0:T(8,128)(2,1)} %bitcast.98, pred[16,8]{0,1:T(8,128)(4,1)S(1)} %copy.76, f32[8,2,128,128]{2,3,0,1:T(8,128)} %get-tuple-element.945, bf16[16,128,128]{1,2,0:T(8,128)(2,1)S(1)} %bitcast.100, bf16[16,2]{0,1:T(2,128)(2,1)S(1)} %and_convert_fusion.7, pred[]{:T(512)S(6)} %compare.59), kind=kOutput, calls=%fused_computation.53.clone.clone.1 | convolution fusion | flops 1078460416 | bytes 6815937 | tf_op jit(solution)/shard_map/while/body/eval_jaxpr/nrxy,njyz->rjxz/dot_general | solution.py:70
  246.8 7.3 %gather_fusion.1 = bf16[128,128,128]{2,1,0:T(8,128)(2,1)} fusion(bf16[337,128,128]{2,1,0:T(8,128)(2,1)} %get-tuple-element.963, s32[1024]{0:T(1024)S(1)} %pad_clamp_fusion.9), kind=kCustom, calls=%fused_computation.2.clone.clone.clone.1 | custom fusion | bytes 8389120 | tf_op jit(solution)/shard_map/while/body/eval_jaxpr/jit(_take)/gather | solution.py:65
  254.2 4.8 %fusion.105 = f32[8,2,128,128]{2,3,0,1:T(8,128)} fusion(bf16[16,8,128,128]{3,2,1,0:T(8,128)(2,1)} %bitcast.98, pred[16,8]{0,1:T(8,128)(4,1)S(1)} %copy.76, f32[8,2,128,128]{2,3,0,1:T(8,128)} %get-tuple-element.945, bf16[16,128,128]{1,2,0:T(8,128)(2,1)S(1)} %bitcast.100, bf16[16,2]{0,1:T(2,128)(2,1)S(1)} %and_convert_fusion.7, pred[]{:T(512)S(6)} %compare.59), kind=kOutput, calls=%fused_computation.53.clone.clone.1 | convolution fusion | flops 1078460416 | bytes 6815937 | tf_op jit(solution)/shard_map/while/body/eval_jaxpr/nrxy,njyz->rjxz/dot_general | solution.py:70
  259.1 1.6 copy.40
  261.2 0.7 fusion.54
  (216 shorter events, 18.4 us)
Async XLA Ops:
  7.2 18.2 %copy-start = (s32[8,32,2]{1,2,0:T(2,128)S(1)}, s32[8,32,2]{1,2,0:T(2,128)}, u32[]{:S(2)}) copy-start(s32[8,32,2]{1,2,0:T(2,128)} %param.16) | copy-start | bytes 6148
  7.2 17.6 %copy-start.3 = (s32[8,32]{1,0:T(8,128)S(1)}, s32[8,32]{1,0:T(8,128)}, u32[]{:S(2)}) copy-start(s32[8,32]{1,0:T(8,128)} %param.15) | copy-start | bytes 3076
  7.2 70.1 %all-gather.2.cloned.1.call-start = ((), (), s32[]{:S(2)}) async-start(), calls=%async_computation.2 | async-start | bytes 12386304 | tf_op jit(solution)/shard_map/all_gather | solution.py:45
  10.8 77.2 %all-to-all-start = ((bf16[32,1,1,2,128,128]{4,5,3,2,1,0:T(8,128)(2,1)}), bf16[32,1,1,2,128,128]{4,5,3,2,1,0:T(8,128)(2,1)S(1)}, u32[]{:S(2)}, u32[]{:S(2)}) async-start(bf16[32,1,1,2,128,128]{4,5,3,2,1,0:T(8,128)(2,1)} %broadcast_in_dim.199), calls=%async_computation | async-start | bytes 4194304 | tf_op jit(solution)/shard_map/all_to_all | solution.py:20
  24.7 63.2 %copy-start.1 = (s32[8,42]{1,0:T(8,128)}, s32[8,42]{1,0:T(8,128)S(1)}, u32[]{:S(2)}) copy-start(s32[8,42]{1,0:T(8,128)S(1)} %fusion.57) | copy-start | bytes 4036
  141.9 13.7 %copy-start.2 = (s32[8,42]{1,0:T(8,128)S(1)}, s32[8,42]{1,0:T(8,128)}, u32[]{:S(2)}) copy-start(s32[8,42]{1,0:T(8,128)} %get-tuple-element.981) | copy-start | bytes 4036
  146.0 58.5 %all-to-all-start.1 = ((bf16[32,1,1,2,128,128]{4,5,3,2,1,0:T(8,128)(2,1)}), bf16[32,1,1,2,128,128]{4,5,3,2,1,0:T(8,128)(2,1)S(1)}, u32[]{:S(2)}, u32[]{:S(2)}) async-start(bf16[32,1,1,2,128,128]{4,5,3,2,1,0:T(8,128)(2,1)} %broadcast_in_dim.207), calls=%async_computation.1 | async-start | bytes 4194304 | tf_op jit(solution)/shard_map/all_to_all | solution.py:20
Sparse Core Ops, SparseCore 0:
  9.8 67.4 all-gather.1
where the time goes:
time: 270 us; the launch traced here: 269 us
  local copies, waits for them, and re-layouts  93.6 us (35%)
  waiting for transfers between devices  92.3 us (34%)
  matrix products  38.2 us (14%)
  starting transfers between devices  21.5 us (8%)
  between operations  14.2 us (5%)
  other arithmetic  8.6 us (3%)
    gather x8, local copies, waits for them, and re-layouts, accumulate(): left_part = jnp.take(padded, picked, axis=0)  58.1 us
    all_gather x1, waiting for transfers between devices, local(): panel_all = lax.all_gather(x_blocks, 'row', axis=0, tiled=True)  48.9 us
    all_to_all x2, waiting for transfers between devices, copy_for_each(): lax.all_to_all(jnp.broadcast_to(array[None], (length, *array.shape)), axi...  42.7 us
    dot_general x8, matrix products, accumulate(): jnp.einsum('nrxy,njyz->rjxz', left_part, placed, preferred_element_type=j...  38.2 us
    all_to_all x2, starting transfers between devices, copy_for_each(): lax.all_to_all(jnp.broadcast_to(array[None], (length, *array.shape)), axi...  21.4 us
    concatenate x1, local copies, waits for them, and re-layouts, local(): jnp.concatenate([stacked, jnp.zeros((1, block_size, block_size), stacked....  10.6 us
  transfers between devices with their start and end apart: 3, of which 2 were waited for; matrix products, arithmetic and copies ran while one was open for 9% of the time, Pallas kernels for 0%

commit v1 on v0

--- a/solution.py
+++ b/solution.py
@@ -7,6 +7,27 @@
 RB = 8
 JW = 2
 CAPW = 2
+
+
+def collect(shard, axis, dim):
+    devices, position, span = (lax.axis_size(axis), lax.axis_index(axis), shard.shape[dim])
+    upward = [(i, (i + 1) % devices) for i in range(devices)]
+    behind = [(i, (i - 1) % devices) for i in range(devices)]
+    filled = jnp.zeros((*shard.shape[:dim], devices * span, *shard.shape[dim + 1 :]), shard.dtype)
+    filled = lax.dynamic_update_slice_in_dim(filled, shard, position * span, axis=dim)
+    from_left = from_right = shard
+    half = devices // 2
+    for hop in range(1, half + 1):
+        from_left = lax.ppermute(from_left, axis, upward)
+        filled = lax.dynamic_update_slice_in_dim(
+            filled, from_left, (position - hop) % devices * span, axis=dim
+        )
+        if hop < devices - half:
+            from_right = lax.ppermute(from_right, axis, behind)
+            filled = lax.dynamic_update_slice_in_dim(
+                filled, from_right, (position + hop) % devices * span, axis=dim
+            )
+    return filled
 
 
 def laid_out(pieces, dim):
@@ -42,7 +63,7 @@
     block_size = x_blocks.shape[3]
     order_blocks = RB * col_total
     tile_width = order_blocks // row_total
-    panel_all = lax.all_gather(x_blocks, "row", axis=0, tiled=True)
+    panel_all = collect(x_blocks, "row", 0)
     stacked = panel_all.reshape(row_total * capacity, block_size, block_size)
     padded = jnp.concatenate(
         [stacked, jnp.zeros((1, block_size, block_size), stacked.dtype)], axis=0

time: 270 us -> 256 us (0.948)
  the two profiles are of different devices: /device:TPU:1 before, /device:TPU:27 now
where the time goes in v1:
time: 256 us; the launch traced here: 255 us
  local copies, waits for them, and re-layouts  101 us (39%)
  waiting for transfers between devices  81.2 us (32%)
  matrix products  32.2 us (13%)
  starting transfers between devices  29.4 us (11%)
  other arithmetic  8.69 us (3%)
    gather x8, local copies, waits for them, and re-layouts, accumulate(): left_part = jnp.take(padded, picked, axis=0)  57.3 us
    all_to_all x2, waiting for transfers between devices, copy_for_each(): lax.all_to_all(jnp.broadcast_to(array[None], (length, *array.shape)), axi...  45.3 us
    dot_general x8, matrix products, accumulate(): jnp.einsum('nrxy,njyz->rjxz', left_part, placed, preferred_element_type=j...  32.2 us
    ppermute x3, waiting for transfers between devices, collect(): from_right = lax.ppermute(from_right, axis, behind)  20.1 us
    all_to_all x2, starting transfers between devices, copy_for_each(): lax.all_to_all(jnp.broadcast_to(array[None], (length, *array.shape)), axi...  19.2 us
    ppermute x4, waiting for transfers between devices, collect(): from_left = lax.ppermute(from_left, axis, upward)  15.8 us
    ppermute x4, starting transfers between devices, collect(): from_left = lax.ppermute(from_left, axis, upward)  10 us
    concatenate x1, local copies, waits for them, and re-layouts, local(): jnp.concatenate([stacked, jnp.zeros((1, block_size, block_size), stacked....  5.13 us
  transfers between devices with their start and end apart: 9, of which 6 were waited for; matrix products, arithmetic and copies ran while one was open for 12% of the time, Pallas kernels for 0%

profile of v1, /device:TPU:27, one launch (start us, length us, event | category | flops | bytes accessed | tf_op | source)
XLA Modules:
  0.0 254.6 jit_solution(3580214955950441831)
XLA Ops:
  1.4 15.4 %collective-permute-done = bf16[1,1,42,128,128]{4,3,2,1,0:T(8,128)(2,1)S(1)} collective-permute-done((bf16[1,1,42,128,128]{4,3,2,1,0:T(8,128)(2,1)}, bf16[1,1,42,128,128]{4,3,2,1,0:T(8,128)(2,1)S(1)}, u32[]{:S(2)}, u32[]{:S(2)}) %collective-permute-start) | collective-permute-done | bytes 1376288 | tf_op jit(solution)/shard_map/ppermute | solution.py:21
  16.7 3.6 %collective-permute-start.2 = (bf16[1,1,42,128,128]{4,3,2,1,0:T(8,128)(2,1)S(1)}, bf16[1,1,42,128,128]{4,3,2,1,0:T(8,128)(2,1)}, u32[]{:S(2)}, u32[]{:S(2)}) collective-permute-start(bf16[1,1,42,128,128]{4,3,2,1,0:T(8,128)(2,1)S(1)} %collective-permute-done), channel_id=1, source_target_pairs={{0,32},{32,64},{64,96},{96,128},{128,160},{160,192},{192,224},{224... | collective-permute-start | bytes 4128776 | tf_op jit(solution)/shard_map/ppermute | solution.py:21
  21.3 1.8 broadcast_in_dim.202
  23.1 11.1 %all-to-all-start = ((bf16[32,1,1,2,128,128]{4,5,3,2,1,0:T(8,128)(2,1)}), bf16[32,1,1,2,128,128]{4,5,3,2,1,0:T(8,128)(2,1)}, u32[]{:S(2)}, u32[]{:S(2)}) async-start(bf16[32,1,1,2,128,128]{4,5,3,2,1,0:T(8,128)(2,1)} %broadcast_in_dim.202), calls=%async_computation | async-start | bytes 4194304 | tf_op jit(solution)/shard_map/all_to_all | solution.py:41
  38.9 2.9 %collective-permute-start.4 = (bf16[1,1,42,128,128]{4,3,2,1,0:T(8,128)(2,1)}, bf16[1,1,42,128,128]{4,3,2,1,0:T(8,128)(2,1)}, u32[]{:S(2)}, u32[]{:S(2)}) collective-permute-start(bf16[1,1,42,128,128]{4,3,2,1,0:T(8,128)(2,1)} %collective-permute-done.2), channel_id=1, source_target_pairs={{0,32},{32,64},{64,96},{96,128},{128,160},{160,192},{192,224},{224... | collective-permute-start | bytes 4128776 | tf_op jit(solution)/shard_map/ppermute | solution.py:21
  43.2 2.8 %broadcast_in_dim.203 = bf16[8,1,42,128,128]{4,3,2,0,1:T(8,128)(2,1)S(1)} broadcast(bf16[]{:T(256)} %constant.452.clone.1), dimensions={} | broadcast | bytes 11010050 | tf_op jit(solution)/shard_map/broadcast_in_dim | solution.py:16
  46.2 11.4 %collective-permute-done.3 = bf16[1,1,42,128,128]{4,3,2,1,0:T(8,128)(2,1)} collective-permute-done((bf16[1,1,42,128,128]{4,3,2,1,0:T(8,128)(2,1)}, bf16[1,1,42,128,128]{4,3,2,1,0:T(8,128)(2,1)}, u32[]{:S(2)}, u32[]{:S(2)}) %collective-permute-start.3) | collective-permute-done | bytes 1376288 | tf_op jit(solution)/shard_map/ppermute | solution.py:26
  59.3 3.0 %collective-permute-start.6 = (bf16[1,1,42,128,128]{4,3,2,1,0:T(8,128)(2,1)}, bf16[1,1,42,128,128]{4,3,2,1,0:T(8,128)(2,1)S(1)}, u32[]{:S(2)}, u32[]{:S(2)}) collective-permute-start(bf16[1,1,42,128,128]{4,3,2,1,0:T(8,128)(2,1)} %collective-permute-done.4), channel_id=1, source_target_pairs={{0,32},{32,64},{64,96},{96,128},{128,160},{160,192},{192,224},{224... | collective-permute-start | bytes 4128776 | tf_op jit(solution)/shard_map/ppermute | solution.py:21
  68.6 8.6 %collective-permute-done.5 = bf16[1,1,42,128,128]{4,3,2,1,0:T(8,128)(2,1)S(1)} collective-permute-done((bf16[1,1,42,128,128]{4,3,2,1,0:T(8,128)(2,1)}, bf16[1,1,42,128,128]{4,3,2,1,0:T(8,128)(2,1)S(1)}, u32[]{:S(2)}, u32[]{:S(2)}) %collective-permute-start.5) | collective-permute-done | bytes 1376288 | tf_op jit(solution)/shard_map/ppermute | solution.py:26
  78.0 5.1 %concatenate.3 = bf16[337,128,128]{2,1,0:T(8,128)(2,1)} pad(bf16[336,128,128]{2,1,0:T(8,128)(2,1)S(1)} %bitcast.115, bf16[]{:T(256)} %constant.452.clone.1), padding=0_1x0_0x0_0 | pad | bytes 22052866 | tf_op jit(solution)/shard_map/concatenate | solution.py:68
  84.2 51.9 %while.36 = (s32[]{:T(128)}, f32[8,2,128,128]{2,3,0,1:T(8,128)S(1)}, s32[32,42]{1,0:T(8,128)S(1)}, s32[32]{0:T(128)S(1)}, bf16[1,32,2,128,128]{3,4,2,1,0:T(8,128...) while((s32[]{:T(128)}, ...), condition=%wide.wide.region_2.4_spmd.clone, body=%wide.wide.region_0.3_spmd.clone.sunk | while | flops 1078636672 | bytes 16272037 | solution.py:125
  85.3 7.2 %gather_fusion = bf16[128,128,128]{2,1,0:T(8,128)(2,1)} fusion(bf16[337,128,128]{2,1,0:T(8,128)(2,1)} %get-tuple-element.924, s32[1024]{0:T(1024)S(1)} %pad_clamp_fusion.8), kind=kCustom, calls=%fused_computation.clone.clone.clone.1 | custom fusion | bytes 8389120 | tf_op jit(solution)/shard_map/while/body/eval_jaxpr/jit(_take)/gather | solution.py:86
  93.9 3.3 %fusion.100 = f32[8,2,128,128]{2,3,0,1:T(8,128)S(1)} fusion(bf16[16,8,128,128]{3,2,1,0:T(8,128)(2,1)} %bitcast.113, pred[16,8]{0,1:T(8,128)(4,1)S(1)} %copy.105, f32[8,2,128,128]{2,3,0,1:T(8,128)S(1)} %get-tuple-element.906, bf16[16,128,128]{1,2,0:T(8,128)(2,1)S(1)} %bitcast.116, bf16[16,2]{0,1:T(2,128)(2,1)S(1)} %and_convert_fusion.6, ...), kind=kOutput, calls=%fused_computation.17.clone.clone.1 | convolution fusion | flops 1078460416 | bytes 6815937 | tf_op jit(solution)/shard_map/while/body/eval_jaxpr/nrxy,njyz->rjxz/dot_general | solution.py:91
  98.3 7.2 %gather_fusion = bf16[128,128,128]{2,1,0:T(8,128)(2,1)} fusion(bf16[337,128,128]{2,1,0:T(8,128)(2,1)} %get-tuple-element.924, s32[1024]{0:T(1024)S(1)} %pad_clamp_fusion.8), kind=kCustom, calls=%fused_computation.clone.clone.clone.1 | custom fusion | bytes 8389120 | tf_op jit(solution)/shard_map/while/body/eval_jaxpr/jit(_take)/gather | solution.py:86
  106.9 3.3 %fusion.100 = f32[8,2,128,128]{2,3,0,1:T(8,128)S(1)} fusion(bf16[16,8,128,128]{3,2,1,0:T(8,128)(2,1)} %bitcast.113, pred[16,8]{0,1:T(8,128)(4,1)S(1)} %copy.105, f32[8,2,128,128]{2,3,0,1:T(8,128)S(1)} %get-tuple-element.906, bf16[16,128,128]{1,2,0:T(8,128)(2,1)S(1)} %bitcast.116, bf16[16,2]{0,1:T(2,128)(2,1)S(1)} %and_convert_fusion.6, ...), kind=kOutput, calls=%fused_computation.17.clone.clone.1 | convolution fusion | flops 1078460416 | bytes 6815937 | tf_op jit(solution)/shard_map/while/body/eval_jaxpr/nrxy,njyz->rjxz/dot_general | solution.py:91
  111.3 7.2 %gather_fusion = bf16[128,128,128]{2,1,0:T(8,128)(2,1)} fusion(bf16[337,128,128]{2,1,0:T(8,128)(2,1)} %get-tuple-element.924, s32[1024]{0:T(1024)S(1)} %pad_clamp_fusion.8), kind=kCustom, calls=%fused_computation.clone.clone.clone.1 | custom fusion | bytes 8389120 | tf_op jit(solution)/shard_map/while/body/eval_jaxpr/jit(_take)/gather | solution.py:86
  119.8 3.3 %fusion.100 = f32[8,2,128,128]{2,3,0,1:T(8,128)S(1)} fusion(bf16[16,8,128,128]{3,2,1,0:T(8,128)(2,1)} %bitcast.113, pred[16,8]{0,1:T(8,128)(4,1)S(1)} %copy.105, f32[8,2,128,128]{2,3,0,1:T(8,128)S(1)} %get-tuple-element.906, bf16[16,128,128]{1,2,0:T(8,128)(2,1)S(1)} %bitcast.116, bf16[16,2]{0,1:T(2,128)(2,1)S(1)} %and_convert_fusion.6, ...), kind=kOutput, calls=%fused_computation.17.clone.clone.1 | convolution fusion | flops 1078460416 | bytes 6815937 | tf_op jit(solution)/shard_map/while/body/eval_jaxpr/nrxy,njyz->rjxz/dot_general | solution.py:91
  124.3 7.2 %gather_fusion = bf16[128,128,128]{2,1,0:T(8,128)(2,1)} fusion(bf16[337,128,128]{2,1,0:T(8,128)(2,1)} %get-tuple-element.924, s32[1024]{0:T(1024)S(1)} %pad_clamp_fusion.8), kind=kCustom, calls=%fused_computation.clone.clone.clone.1 | custom fusion | bytes 8389120 | tf_op jit(solution)/shard_map/while/body/eval_jaxpr/jit(_take)/gather | solution.py:86
  132.8 3.3 %fusion.100 = f32[8,2,128,128]{2,3,0,1:T(8,128)S(1)} fusion(bf16[16,8,128,128]{3,2,1,0:T(8,128)(2,1)} %bitcast.113, pred[16,8]{0,1:T(8,128)(4,1)S(1)} %copy.105, f32[8,2,128,128]{2,3,0,1:T(8,128)S(1)} %get-tuple-element.906, bf16[16,128,128]{1,2,0:T(8,128)(2,1)S(1)} %bitcast.116, bf16[16,2]{0,1:T(2,128)(2,1)S(1)} %and_convert_fusion.6, ...), kind=kOutput, calls=%fused_computation.17.clone.clone.1 | convolution fusion | flops 1078460416 | bytes 6815937 | tf_op jit(solution)/shard_map/while/body/eval_jaxpr/nrxy,njyz->rjxz/dot_general | solution.py:91
  137.2 1.9 broadcast_in_dim.211
  139.1 8.1 %all-to-all-start.1 = ((bf16[32,1,1,2,128,128]{4,5,3,2,1,0:T(8,128)(2,1)}), bf16[32,1,1,2,128,128]{4,5,3,2,1,0:T(8,128)(2,1)S(1)}, u32[]{:S(2)}, u32[]{:S(2)}) async-start(bf16[32,1,1,2,128,128]{4,5,3,2,1,0:T(8,128)(2,1)} %broadcast_in_dim.211), calls=%async_computation.1 | async-start | bytes 4194304 | tf_op jit(solution)/shard_map/all_to_all | solution.py:41
  148.0 4.7 %gather_fusion.2 = bf16[2,128,128]{2,1,0:T(8,128)(2,1)S(1)} fusion(bf16[337,128,128]{2,1,0:T(8,128)(2,1)} %get-tuple-element.970, s32[1024]{0:T(1024)S(1)} %pad_clamp_fusion.2), kind=kCustom, calls=%fused_computation.4 | custom fusion | bytes 131080 | tf_op jit(solution)/shard_map/jit(_take)/gather | solution.py:145
  153.4 44.2 %all-to-all-done.1 = bf16[32,1,1,2,128,128]{4,5,3,2,1,0:T(8,128)(2,1)S(1)} async-done(((bf16[32,1,1,2,128,128]{4,5,3,2,1,0:T(8,128)(2,1)}), bf16[32,1,1,2,128,128]{4,5,3,2,1,0:T(8,128)(2,1)S(1)}, u32[]{:S(2)}, u32[]{:S(2)}) %all-to-all-start.1) | async-done | bytes 2097184 | tf_op jit(solution)/shard_map/all_to_all | solution.py:41
  197.7 54.1 %while.37 = (s32[]{:T(128)}, f32[8,2,128,128]{2,3,0,1:T(8,128)}, s32[32,2]{0,1:T(2,128)S(1)}, s32[32]{0:T(128)S(1)}, bf16[1,32,2,128,128]{3,4,2,1,0:T(8,128)(2,1...) while((s32[]{:T(128)}, f32[8,2,128,128]{2,3,0,1:T(8,128)}, ...), condition=%wide.wide.region_6.9_spmd.clone, body=%wide.wide.region_4.8_spmd.clone.sunk | while | flops 1078636672 | bytes 16269573 | solution.py:125
  199.1 7.2 %gather_fusion.1 = bf16[128,128,128]{2,1,0:T(8,128)(2,1)} fusion(bf16[337,128,128]{2,1,0:T(8,128)(2,1)} %get-tuple-element.963, s32[1024]{0:T(1024)S(1)} %pad_clamp_fusion.9), kind=kCustom, calls=%fused_computation.2.clone.clone.clone.1 | custom fusion | bytes 8389120 | tf_op jit(solution)/shard_map/while/body/eval_jaxpr/jit(_take)/gather | solution.py:86
  206.4 4.5 %fusion.105 = f32[8,2,128,128]{2,3,0,1:T(8,128)} fusion(bf16[16,8,128,128]{3,2,1,0:T(8,128)(2,1)} %bitcast.114, pred[16,8]{0,1:T(8,128)(4,1)S(1)} %copy.108, f32[8,2,128,128]{2,3,0,1:T(8,128)} %get-tuple-element.945, bf16[16,128,128]{1,2,0:T(8,128)(2,1)S(1)} %bitcast.117, bf16[16,2]{0,1:T(2,128)(2,1)S(1)} %and_convert_fusion.7, pred[]{:T(512)S(6)} %compare.66), kind=kOutput, calls=%fused_computation.53.clone.clone.1 | convolution fusion | flops 1078460416 | bytes 6815937 | tf_op jit(solution)/shard_map/while/body/eval_jaxpr/nrxy,njyz->rjxz/dot_general | solution.py:91
  212.4 7.2 %gather_fusion.1 = bf16[128,128,128]{2,1,0:T(8,128)(2,1)} fusion(bf16[337,128,128]{2,1,0:T(8,128)(2,1)} %get-tuple-element.963, s32[1024]{0:T(1024)S(1)} %pad_clamp_fusion.9), kind=kCustom, calls=%fused_computation.2.clone.clone.clone.1 | custom fusion | bytes 8389120 | tf_op jit(solution)/shard_map/while/body/eval_jaxpr/jit(_take)/gather | solution.py:86
  219.7 4.8 %fusion.105 = f32[8,2,128,128]{2,3,0,1:T(8,128)} fusion(bf16[16,8,128,128]{3,2,1,0:T(8,128)(2,1)} %bitcast.114, pred[16,8]{0,1:T(8,128)(4,1)S(1)} %copy.108, f32[8,2,128,128]{2,3,0,1:T(8,128)} %get-tuple-element.945, bf16[16,128,128]{1,2,0:T(8,128)(2,1)S(1)} %bitcast.117, bf16[16,2]{0,1:T(2,128)(2,1)S(1)} %and_convert_fusion.7, pred[]{:T(512)S(6)} %compare.66), kind=kOutput, calls=%fused_computation.53.clone.clone.1 | convolution fusion | flops 1078460416 | bytes 6815937 | tf_op jit(solution)/shard_map/while/body/eval_jaxpr/nrxy,njyz->rjxz/dot_general | solution.py:91
  226.0 7.2 %gather_fusion.1 = bf16[128,128,128]{2,1,0:T(8,128)(2,1)} fusion(bf16[337,128,128]{2,1,0:T(8,128)(2,1)} %get-tuple-element.963, s32[1024]{0:T(1024)S(1)} %pad_clamp_fusion.9), kind=kCustom, calls=%fused_computation.2.clone.clone.clone.1 | custom fusion | bytes 8389120 | tf_op jit(solution)/shard_map/while/body/eval_jaxpr/jit(_take)/gather | solution.py:86
  233.3 4.8 %fusion.105 = f32[8,2,128,128]{2,3,0,1:T(8,128)} fusion(bf16[16,8,128,128]{3,2,1,0:T(8,128)(2,1)} %bitcast.114, pred[16,8]{0,1:T(8,128)(4,1)S(1)} %copy.108, f32[8,2,128,128]{2,3,0,1:T(8,128)} %get-tuple-element.945, bf16[16,128,128]{1,2,0:T(8,128)(2,1)S(1)} %bitcast.117, bf16[16,2]{0,1:T(2,128)(2,1)S(1)} %and_convert_fusion.7, pred[]{:T(512)S(6)} %compare.66), kind=kOutput, calls=%fused_computation.53.clone.clone.1 | convolution fusion | flops 1078460416 | bytes 6815937 | tf_op jit(solution)/shard_map/while/body/eval_jaxpr/nrxy,njyz->rjxz/dot_general | solution.py:91
  239.6 7.2 %gather_fusion.1 = bf16[128,128,128]{2,1,0:T(8,128)(2,1)} fusion(bf16[337,128,128]{2,1,0:T(8,128)(2,1)} %get-tuple-element.963, s32[1024]{0:T(1024)S(1)} %pad_clamp_fusion.9), kind=kCustom, calls=%fused_computation.2.clone.clone.clone.1 | custom fusion | bytes 8389120 | tf_op jit(solution)/shard_map/while/body/eval_jaxpr/jit(_take)/gather | solution.py:86
  246.9 4.8 %fusion.105 = f32[8,2,128,128]{2,3,0,1:T(8,128)} fusion(bf16[16,8,128,128]{3,2,1,0:T(8,128)(2,1)} %bitcast.114, pred[16,8]{0,1:T(8,128)(4,1)S(1)} %copy.108, f32[8,2,128,128]{2,3,0,1:T(8,128)} %get-tuple-element.945, bf16[16,128,128]{1,2,0:T(8,128)(2,1)S(1)} %bitcast.117, bf16[16,2]{0,1:T(2,128)(2,1)S(1)} %and_convert_fusion.7, pred[]{:T(512)S(6)} %compare.66), kind=kOutput, calls=%fused_computation.53.clone.clone.1 | convolution fusion | flops 1078460416 | bytes 6815937 | tf_op jit(solution)/shard_map/while/body/eval_jaxpr/nrxy,njyz->rjxz/dot_general | solution.py:91
  (242 shorter events, 38.8 us)
Async XLA Ops:
  0.6 34.0 %copy-start = (s32[8,32,2]{1,2,0:T(2,128)S(1)}, s32[8,32,2]{1,2,0:T(2,128)}, u32[]{:S(2)}) copy-start(s32[8,32,2]{1,2,0:T(2,128)} %param.16) | copy-start | bytes 6148
  0.6 33.6 %copy-start.6 = (s32[8,32]{1,0:T(8,128)S(1)}, s32[8,32]{1,0:T(8,128)}, u32[]{:S(2)}) copy-start(s32[8,32]{1,0:T(8,128)} %param.15) | copy-start | bytes 3076
  0.7 16.1 %collective-permute-start = (bf16[1,1,42,128,128]{4,3,2,1,0:T(8,128)(2,1)}, bf16[1,1,42,128,128]{4,3,2,1,0:T(8,128)(2,1)S(1)}, u32[]{:S(2)}, u32[]{:S(2)}) collective-permute-start(bf16[1,1,42,128,128]{4,3,2,1,0:T(8,128)(2,1)} %param.13), channel_id=1, source_target_pairs={{0,32},{32,64},{64,96},{96,128},{128,160},{160,192},{192,224},{224... | collective-permute-start | bytes 4128776 | tf_op jit(solution)/shard_map/ppermute | solution.py:21
  1.2 36.9 %collective-permute-start.1 = (bf16[1,1,42,128,128]{4,3,2,1,0:T(8,128)(2,1)}, bf16[1,1,42,128,128]{4,3,2,1,0:T(8,128)(2,1)}, u32[]{:S(2)}, u32[]{:S(2)}) collective-permute-start(bf16[1,1,42,128,128]{4,3,2,1,0:T(8,128)(2,1)} %param.13), channel_id=1, source_target_pairs={{0,224},{32,0},{64,32},{96,64},{128,96},{160,128},{192,160},{224,1... | collective-permute-start | bytes 4128776 | tf_op jit(solution)/shard_map/ppermute | solution.py:26
  16.7 26.4 %copy-start.2 = (bf16[1,1,42,128,128]{4,3,2,1,0:T(8,128)(2,1)}, bf16[1,1,42,128,128]{4,3,2,1,0:T(8,128)(2,1)S(1)}, u32[]{:S(2)}) copy-start(bf16[1,1,42,128,128]{4,3,2,1,0:T(8,128)(2,1)S(1)} %collective-permute-done) | copy-start | bytes 4128772
  16.7 22.1 %collective-permute-start.2 = (bf16[1,1,42,128,128]{4,3,2,1,0:T(8,128)(2,1)S(1)}, bf16[1,1,42,128,128]{4,3,2,1,0:T(8,128)(2,1)}, u32[]{:S(2)}, u32[]{:S(2)}) collective-permute-start(bf16[1,1,42,128,128]{4,3,2,1,0:T(8,128)(2,1)S(1)} %collective-permute-done), channel_id=1, source_target_pairs={{0,32},{32,64},{64,96},{96,128},{128,160},{160,192},{192,224},{224... | collective-permute-start | bytes 4128776 | tf_op jit(solution)/shard_map/ppermute | solution.py:21
  23.1 61.1 %all-to-all-start = ((bf16[32,1,1,2,128,128]{4,5,3,2,1,0:T(8,128)(2,1)}), bf16[32,1,1,2,128,128]{4,5,3,2,1,0:T(8,128)(2,1)}, u32[]{:S(2)}, u32[]{:S(2)}) async-start(bf16[32,1,1,2,128,128]{4,5,3,2,1,0:T(8,128)(2,1)} %broadcast_in_dim.202), calls=%async_computation | async-start | bytes 4194304 | tf_op jit(solution)/shard_map/all_to_all | solution.py:41
  38.1 19.6 %collective-permute-start.3 = (bf16[1,1,42,128,128]{4,3,2,1,0:T(8,128)(2,1)}, bf16[1,1,42,128,128]{4,3,2,1,0:T(8,128)(2,1)}, u32[]{:S(2)}, u32[]{:S(2)}) collective-permute-start(bf16[1,1,42,128,128]{4,3,2,1,0:T(8,128)(2,1)} %collective-permute-done.1), channel_id=1, source_target_pairs={{0,224},{32,0},{64,32},{96,64},{128,96},{160,128},{192,160},{224,1... | collective-permute-start | bytes 4128776 | tf_op jit(solution)/shard_map/ppermute | solution.py:26
  38.8 7.1 %copy-start.4 = (s32[8,42]{1,0:T(8,128)}, s32[8,42]{1,0:T(8,128)S(1)}, u32[]{:S(2)}) copy-start(s32[8,42]{1,0:T(8,128)S(1)} %fusion.57) | copy-start | bytes 4036
  38.9 20.4 %collective-permute-start.4 = (bf16[1,1,42,128,128]{4,3,2,1,0:T(8,128)(2,1)}, bf16[1,1,42,128,128]{4,3,2,1,0:T(8,128)(2,1)}, u32[]{:S(2)}, u32[]{:S(2)}) collective-permute-start(bf16[1,1,42,128,128]{4,3,2,1,0:T(8,128)(2,1)} %collective-permute-done.2), channel_id=1, source_target_pairs={{0,32},{32,64},{64,96},{96,128},{128,160},{160,192},{192,224},{224... | collective-permute-start | bytes 4128776 | tf_op jit(solution)/shard_map/ppermute | solution.py:21
  43.2 2.8 %copy-start.1 = (bf16[1,1,42,128,128]{4,3,2,1,0:T(8,128)(2,1)S(1)}, bf16[1,1,42,128,128]{4,3,2,1,0:T(8,128)(2,1)}, u32[]{:S(2)}) copy-start(bf16[1,1,42,128,128]{4,3,2,1,0:T(8,128)(2,1)} %param.13) | copy-start | bytes 4128772
  57.7 19.6 %collective-permute-start.5 = (bf16[1,1,42,128,128]{4,3,2,1,0:T(8,128)(2,1)}, bf16[1,1,42,128,128]{4,3,2,1,0:T(8,128)(2,1)S(1)}, u32[]{:S(2)}, u32[]{:S(2)}) collective-permute-start(bf16[1,1,42,128,128]{4,3,2,1,0:T(8,128)(2,1)} %collective-permute-done.3), channel_id=1, source_target_pairs={{0,224},{32,0},{64,32},{96,64},{128,96},{160,128},{192,160},{224,1... | collective-permute-start | bytes 4128776 | tf_op jit(solution)/shard_map/ppermute | solution.py:26
  59.3 18.5 %collective-permute-start.6 = (bf16[1,1,42,128,128]{4,3,2,1,0:T(8,128)(2,1)}, bf16[1,1,42,128,128]{4,3,2,1,0:T(8,128)(2,1)S(1)}, u32[]{:S(2)}, u32[]{:S(2)}) collective-permute-start(bf16[1,1,42,128,128]{4,3,2,1,0:T(8,128)(2,1)} %collective-permute-done.4), channel_id=1, source_target_pairs={{0,32},{32,64},{64,96},{96,128},{128,160},{160,192},{192,224},{224... | collective-permute-start | bytes 4128776 | tf_op jit(solution)/shard_map/ppermute | solution.py:21
  78.0 6.3 %copy-start.3 = (f32[8,2,128,128]{2,3,0,1:T(8,128)S(1)}, f32[8,2,128,128]{2,3,0,1:T(8,128)}, u32[]{:S(2)}) copy-start(f32[8,2,128,128]{2,3,0,1:T(8,128)} %custom-call) | copy-start | bytes 3145732
  136.2 11.1 %copy-start.5 = (s32[8,42]{1,0:T(8,128)S(1)}, s32[8,42]{1,0:T(8,128)}, u32[]{:S(2)}) copy-start(s32[8,42]{1,0:T(8,128)} %get-tuple-element.980) | copy-start | bytes 4036
  139.1 58.6 %all-to-all-start.1 = ((bf16[32,1,1,2,128,128]{4,5,3,2,1,0:T(8,128)(2,1)}), bf16[32,1,1,2,128,128]{4,5,3,2,1,0:T(8,128)(2,1)S(1)}, u32[]{:S(2)}, u32[]{:S(2)}) async-start(bf16[32,1,1,2,128,128]{4,5,3,2,1,0:T(8,128)(2,1)} %broadcast_in_dim.211), calls=%async_computation.1 | async-start | bytes 4194304 | tf_op jit(solution)/shard_map/all_to_all | solution.py:41
